TPU v7x, 32 devices: a whole 2x2x4 slice. The times are simulated.
32 devices in a mesh: elem: 8 (over z, y), chan: 4 (over x, core).
Axes of the slice: x: 2, y: 2, z: 4, core: 2. Of those that a mesh axis runs over, the one named last changes fastest.
Arguments:
- voltages: bfloat16 [2, 1024, 19584], P(None, ('elem', 'chan')), may hold values from -6 to 6
- delays: int32 [1024], P(('elem', 'chan')), may hold values from 0 to 127
- prototype: bfloat16 [16, 1024], replicated, may hold values from -1.5 to 1.5
- subband_map: int32 [16], replicated, may hold values from 0 to 1023, as said below
- beam_weights: bfloat16 [512, 2, 16, 1024], P('elem', None, 'chan'), may hold values from -0.25 to 0.25
Outputs:
- element_power: bfloat16 [1024, 1024], P(('elem', 'chan'))
- beam_voltages: float32 [2, 64, 512], P(None, 'chan', 'elem')
Inputs may be any that keep to these rules, and one draw needn't show every extreme that they name: `subband_map`: distinct channel numbers.
All inputs are finite; a program needn't handle non-finite values.
Results may differ from a plain program's by a relative error of at most 0.007.
Values may be sent and summed in bfloat16 or wider, within the bound.
A program may use at most 128 MiB of HBM per device.

v0:
```python
import math

import jax
import jax.numpy as jnp
from jax import lax
from jax.sharding import PartitionSpec as P

FRAMES = 4
SUB_C = 4


def filtered(voltages, delays, prototype):
    tap_count, chan_count = prototype.shape
    blocks = FRAMES + tap_count - 1
    window_len = blocks * chan_count

    def window(samples, offset):
        return lax.dynamic_slice_in_dim(samples, offset, window_len, 0)

    segments = jax.vmap(jax.vmap(window, in_axes=(0, 0)), in_axes=(0, None))(voltages, delays)
    segments = segments.reshape(voltages.shape[0], voltages.shape[1], blocks, chan_count)
    coeffs = prototype.astype(jnp.float32)
    running = jnp.zeros((voltages.shape[0], voltages.shape[1], FRAMES, chan_count), jnp.float32)
    for tap_index in range(tap_count):
        running = running + coeffs[tap_index] * segments[
            :, :, tap_index : tap_index + FRAMES, :
        ].astype(jnp.float32)
    return running.astype(jnp.bfloat16)


def spectra(filtered_wave):
    part_count, elem_count, frame_count, chan_count = filtered_wave.shape
    counter = jnp.arange(chan_count, dtype=jnp.int32)
    residue = counter[:, None] * counter[None, :] % chan_count
    radians = residue.astype(jnp.float32) * (2.0 * math.pi / chan_count)
    factor = 1.0 / math.sqrt(chan_count)
    basis = jnp.concatenate([jnp.cos(radians) * factor, jnp.sin(radians) * factor], axis=1)
    basis_high = basis.astype(jnp.bfloat16)
    basis_low = (basis - basis_high.astype(jnp.float32)).astype(jnp.bfloat16)
    flattened = filtered_wave.reshape(part_count * elem_count * frame_count, chan_count)
    product = jnp.dot(flattened, basis_high, preferred_element_type=jnp.float32)
    product = product + jnp.dot(flattened, basis_low, preferred_element_type=jnp.float32)
    product = product.reshape(part_count, elem_count, frame_count, 2, chan_count)
    spec_real = product[0, :, :, 0] + product[1, :, :, 1]
    spec_imag = product[1, :, :, 0] - product[0, :, :, 1]
    return (spec_real, spec_imag)


def beam_terms(spectra_part, weight_part):
    weight_real = weight_part[:, 0]
    weight_imag = weight_part[:, 1]

    def contract(spectral, weighting):
        return jnp.einsum("sfe,bse->sfb", spectral, weighting, preferred_element_type=jnp.float32)

    out_real = contract(spectra_part[0], weight_real) - contract(spectra_part[1], weight_imag)
    out_imag = contract(spectra_part[1], weight_real) + contract(spectra_part[0], weight_imag)
    return jnp.stack([out_real, out_imag])


def on_device(voltages, delays, prototype, subband_map, beam_weights):
    filtered_wave = filtered(voltages, delays, prototype)
    spec_real, spec_imag = spectra(filtered_wave)
    element_power = jnp.mean(spec_real * spec_real + spec_imag * spec_imag, axis=1).astype(
        jnp.bfloat16
    )
    picked = jnp.stack([spec_real[:, :, subband_map], spec_imag[:, :, subband_map]]).astype(
        jnp.bfloat16
    )
    picked = jnp.transpose(picked, (0, 3, 2, 1))
    turned = lax.all_to_all(picked, "chan", split_axis=1, concat_axis=3, tiled=True)
    local_beams = beam_weights.shape[0]
    summed = beam_terms(lax.all_gather(turned, "elem", axis=3, tiled=True), beam_weights)
    beam_voltages = summed.reshape(2, SUB_C * FRAMES, local_beams)
    return (element_power, beam_voltages)


def solution(mesh):
    return jax.shard_map(
        on_device,
        mesh=mesh,
        in_specs=(
            P(None, ("elem", "chan"), None),
            P(("elem", "chan")),
            P(),
            P(),
            P("elem", None, "chan", None),
        ),
        out_specs=(P(("elem", "chan"), None), P(None, "chan", "elem")),
        check_vma=False,
    )
```

profile of v0, /device:TPU:0, one launch (start us, length us, event | category | flops | bytes accessed | tf_op | source)
XLA Modules:
  0.0 187.4 jit_solution(4113093099833259249)
XLA Ops:
  0.7 17.8 %sine_multiply_fusion = (f32[1024,1024]{1,0:T(8,128)}, f32[1024,1024]{1,0:T(8,128)}) fusion(), kind=kLoop, calls=%fused_computation.14 | loop fusion | flops 16777216 | bytes 8388608 | tf_op jit(solution)/shard_map/mul | solution.py:37
  20.5 85.7 %while.1 = (s32[]{:T(128)}, bf16[2,32,19584]{2,0,1:T(2,128)(2,1)S(1)}, s32[32,2]{0,1:T(2,128)S(1)}, bf16[32,2,19456]{2,1,0:T(2,128)(2,1)}, s32[]{:T(128)}) while((s32[]{:T(128)}, bf16[2,32,19584]{2,0,1:T(2,128)(2,1)S(1)}, s32[32,2]{0,1:T(2,128)S(1)}, bf16[32,2,19456]{2,1,0:T(2,128)(2,1)}, s32[]{:T(128)}) %tuple.49), condition=%wide.while_cond, body=%wide.while_body.sunk | while | flops 2 | bytes 157281 | solution.py:18
  31.9 2.1 %bitcast_dynamic-update-slice_fusion.2 = bf16[32,2,19456]{2,1,0:T(2,128)(2,1)} fusion(bf16[32,2,19456]{2,1,0:T(2,128)(2,1)} %get-tuple-element.97, s32[]{:T(128)} %get-tuple-element.94, bf16[2,32,19584]{2,0,1:T(2,128)(2,1)S(1)} %get-tuple-element.100, s32[]{:T(128)} %bitcast.72, s32[]{:T(128)} %bitcast.73), kind=kLoop, calls=%fused_computation.2.clone.1 | loop fusion | bytes 157184 | tf_op jit(solution)/shard_map/vmap(vmap())/gather
  37.2 2.1 %bitcast_dynamic-update-slice_fusion.2 = bf16[32,2,19456]{2,1,0:T(2,128)(2,1)} fusion(bf16[32,2,19456]{2,1,0:T(2,128)(2,1)} %get-tuple-element.97, s32[]{:T(128)} %get-tuple-element.94, bf16[2,32,19584]{2,0,1:T(2,128)(2,1)S(1)} %get-tuple-element.100, s32[]{:T(128)} %bitcast.72, s32[]{:T(128)} %bitcast.73), kind=kLoop, calls=%fused_computation.2.clone.1 | loop fusion | bytes 157184 | tf_op jit(solution)/shard_map/vmap(vmap())/gather
  39.9 2.1 %bitcast_dynamic-update-slice_fusion.2 = bf16[32,2,19456]{2,1,0:T(2,128)(2,1)} fusion(bf16[32,2,19456]{2,1,0:T(2,128)(2,1)} %get-tuple-element.97, s32[]{:T(128)} %get-tuple-element.94, bf16[2,32,19584]{2,0,1:T(2,128)(2,1)S(1)} %get-tuple-element.100, s32[]{:T(128)} %bitcast.72, s32[]{:T(128)} %bitcast.73), kind=kLoop, calls=%fused_computation.2.clone.1 | loop fusion | bytes 157184 | tf_op jit(solution)/shard_map/vmap(vmap())/gather
  45.3 2.1 %bitcast_dynamic-update-slice_fusion.2 = bf16[32,2,19456]{2,1,0:T(2,128)(2,1)} fusion(bf16[32,2,19456]{2,1,0:T(2,128)(2,1)} %get-tuple-element.97, s32[]{:T(128)} %get-tuple-element.94, bf16[2,32,19584]{2,0,1:T(2,128)(2,1)S(1)} %get-tuple-element.100, s32[]{:T(128)} %bitcast.72, s32[]{:T(128)} %bitcast.73), kind=kLoop, calls=%fused_computation.2.clone.1 | loop fusion | bytes 157184 | tf_op jit(solution)/shard_map/vmap(vmap())/gather
  53.3 2.1 %bitcast_dynamic-update-slice_fusion.2 = bf16[32,2,19456]{2,1,0:T(2,128)(2,1)} fusion(bf16[32,2,19456]{2,1,0:T(2,128)(2,1)} %get-tuple-element.97, s32[]{:T(128)} %get-tuple-element.94, bf16[2,32,19584]{2,0,1:T(2,128)(2,1)S(1)} %get-tuple-element.100, s32[]{:T(128)} %bitcast.72, s32[]{:T(128)} %bitcast.73), kind=kLoop, calls=%fused_computation.2.clone.1 | loop fusion | bytes 157184 | tf_op jit(solution)/shard_map/vmap(vmap())/gather
  58.7 2.1 %bitcast_dynamic-update-slice_fusion.2 = bf16[32,2,19456]{2,1,0:T(2,128)(2,1)} fusion(bf16[32,2,19456]{2,1,0:T(2,128)(2,1)} %get-tuple-element.97, s32[]{:T(128)} %get-tuple-element.94, bf16[2,32,19584]{2,0,1:T(2,128)(2,1)S(1)} %get-tuple-element.100, s32[]{:T(128)} %bitcast.72, s32[]{:T(128)} %bitcast.73), kind=kLoop, calls=%fused_computation.2.clone.1 | loop fusion | bytes 157184 | tf_op jit(solution)/shard_map/vmap(vmap())/gather
  88.1 2.1 %bitcast_dynamic-update-slice_fusion.2 = bf16[32,2,19456]{2,1,0:T(2,128)(2,1)} fusion(bf16[32,2,19456]{2,1,0:T(2,128)(2,1)} %get-tuple-element.97, s32[]{:T(128)} %get-tuple-element.94, bf16[2,32,19584]{2,0,1:T(2,128)(2,1)S(1)} %get-tuple-element.100, s32[]{:T(128)} %bitcast.72, s32[]{:T(128)} %bitcast.73), kind=kLoop, calls=%fused_computation.2.clone.1 | loop fusion | bytes 157184 | tf_op jit(solution)/shard_map/vmap(vmap())/gather
  90.8 2.1 %bitcast_dynamic-update-slice_fusion.2 = bf16[32,2,19456]{2,1,0:T(2,128)(2,1)} fusion(bf16[32,2,19456]{2,1,0:T(2,128)(2,1)} %get-tuple-element.97, s32[]{:T(128)} %get-tuple-element.94, bf16[2,32,19584]{2,0,1:T(2,128)(2,1)S(1)} %get-tuple-element.100, s32[]{:T(128)} %bitcast.72, s32[]{:T(128)} %bitcast.73), kind=kLoop, calls=%fused_computation.2.clone.1 | loop fusion | bytes 157184 | tf_op jit(solution)/shard_map/vmap(vmap())/gather
  101.5 2.1 %bitcast_dynamic-update-slice_fusion.2 = bf16[32,2,19456]{2,1,0:T(2,128)(2,1)} fusion(bf16[32,2,19456]{2,1,0:T(2,128)(2,1)} %get-tuple-element.97, s32[]{:T(128)} %get-tuple-element.94, bf16[2,32,19584]{2,0,1:T(2,128)(2,1)S(1)} %get-tuple-element.100, s32[]{:T(128)} %bitcast.72, s32[]{:T(128)} %bitcast.73), kind=kLoop, calls=%fused_computation.2.clone.1 | loop fusion | bytes 157184 | tf_op jit(solution)/shard_map/vmap(vmap())/gather
  106.2 3.6 %copy.23 = bf16[2,32,19456]{2,1,0:T(8,128)(2,1)} copy(bf16[2,32,19456]{2,0,1:T(2,128)(2,1)} %bitcast.74) | data formatting | bytes 4980736 | tf_op jit(solution)/shard_map/vmap(vmap())/gather | solution.py:18
  109.9 3.3 %reshape.36 = bf16[2,32,19,1024]{3,2,1,0:T(8,128)(2,1)S(1)} reshape(bf16[2,32,19456]{2,1,0:T(8,128)(2,1)} %copy.23) | data formatting | bytes 4980736 | tf_op jit(solution)/shard_map/reshape | solution.py:21
  113.2 5.1 %add_convert_fusion = bf16[2,32,4,1024]{3,2,1,0:T(4,128)(2,1)} fusion(bf16[2,32,19,1024]{3,2,1,0:T(8,128)(2,1)S(1)} %reshape.36, f32[1024]{0:T(1024)S(1)} %bitcast.94, f32[1024]{0:T(1024)S(1)} %bitcast.93, f32[1024]{0:T(1024)S(1)} %bitcast.92, f32[1024]{0:T(1024)S(1)} %bitcast.91, f32[1024]{0:T(1024)S(1)} %bitcast.90, f32[1024]{0:T(1024)S(1)} %bitcast.89, ...), kind=kLoop, calls=%fused_computation.26 | loop fusion | flops 12582912 | bytes 8978432 | tf_op jit(solution)/shard_map/convert_element_type | solution.py:28
  119.5 4.8 %fusion.1 = f32[256,2048]{1,0:T(8,128)S(1)} fusion(bf16[256,1024]{1,0:T(8,128)(2,1)S(1)} %reshape.37, f32[1024,1024]{1,0:T(8,128)} %get-tuple-element.55, f32[1024,1024]{1,0:T(8,128)} %get-tuple-element.56), kind=kOutput, calls=%fused_computation.10 | convolution fusion | flops 1082130432 | bytes 11010048 | tf_op jit(solution)/shard_map/dot_general | solution.py:41
  126.7 2.8 %reshape.38 = f32[2,32,4,2,1024]{4,3,2,1,0:T(2,128)} reshape(f32[256,2048]{1,0:T(8,128)S(1)} %fusion.10) | data formatting | bytes 4194304 | tf_op jit(solution)/shard_map/reshape | solution.py:43
  129.5 5.4 %fusion.17 = (f32[1,32,4,1,1024]{4,3,2,1,0:T(1,128)S(1)}, f32[1,32,4,1,1024]{4,3,2,1,0:T(1,128)S(1)}, f32[1,32,4,1,1024]{4,3,2,1,0:T(1,128)}, f32[1,32,4,1,1024]{4,3,2,1,0:T(1,128)}) fusion(f32[2,32,4,2,1024]{4,3,2,1,0:T(2,128)} %reshape.38), kind=kLoop, calls=%fused_computation.46 | loop fusion | bytes 4194304 | tf_op jit(solution)/shard_map/slice | solution.py:45
  134.9 2.7 %copy.34 = f32[1,32,4,1,1024]{1,2,4,3,0:T(4,128)S(1)} copy(f32[1,32,4,1,1024]{4,3,2,1,0:T(1,128)} %get-tuple-element.36) | data formatting | bytes 1048576
  137.6 3.3 %copy.35 = f32[1,32,4,1,1024]{1,2,4,3,0:T(4,128)} copy(f32[1,32,4,1,1024]{4,3,2,1,0:T(1,128)} %get-tuple-element.35) | data formatting | bytes 1048576
  141.0 2.4 %copy.36 = f32[1,32,4,1,1024]{1,2,4,3,0:T(4,128)} copy(f32[1,32,4,1,1024]{4,3,2,1,0:T(1,128)S(1)} %get-tuple-element.34) | data formatting | bytes 1048576
  143.3 2.4 %copy.37 = f32[1,32,4,1,1024]{1,2,4,3,0:T(4,128)} copy(f32[1,32,4,1,1024]{4,3,2,1,0:T(1,128)S(1)} %get-tuple-element.33) | data formatting | bytes 1048576
  145.8 5.7 %add_reduce_fusion = (f32[32,1024]{0,1:T(8,128)S(1)}, bf16[32,4,1024]{0,1,2:T(4,128)(2,1)}, bf16[32,4,1024]{0,1,2:T(4,128)(2,1)}) fusion(f32[1,32,4,1,1024]{1,2,4,3,0:T(4,128)S(1)} %copy.34, f32[1,32,4,1,1024]{1,2,4,3,0:T(4,128)} %copy.35, f32[1,32,4,1,1024]{1,2,4,3,0:T(4,128)} %copy.36, f32[1,32,4,1,1024]{1,2,4,3,0:T(4,128)} %copy.37), kind=kLoop, calls=%fused_computation.21 | loop fusion | flops 1015808 | bytes 2752512 | tf_op jit(solution)/shard_map/reduce_sum | solution.py:64
  155.8 4.2 %all-to-all-start = ((bf16[4,2,512]{2,1,0:T(2,128)(2,1)}), bf16[4,2,512]{2,1,0:T(2,128)(2,1)S(1)}, u32[]{:S(2)}, u32[]{:S(2)}) async-start(bf16[4,2,512]{2,1,0:T(2,128)(2,1)} %reshape.78), calls=%async_computation | async-start | bytes 16384 | tf_op jit(solution)/shard_map/all_to_all | solution.py:71
  164.0 21.6 %all_gather.3 = bf16[2,4,4,1024]{3,2,1,0:T(4,128)(2,1)S(1)} all-gather(bf16[2,4,4,128]{3,2,1,0:T(4,128)(2,1)S(1)} %all_to_all.16), channel_id=1, replica_groups=mesh['elem'=8,'chan'=4] {'elem'}, dimensions={3}, use_global_device_ids=true | all-gather | bytes 73728 | tf_op jit(solution)/shard_map/all_gather | solution.py:73
  (126 shorter events, 82.7 us)
Async XLA Ops:
  0.6 17.8 %copy-start.3 = (bf16[16,1024]{1,0:T(8,128)(2,1)S(1)}, bf16[16,1024]{1,0:T(8,128)(2,1)}, u32[]{:S(2)}) copy-start(bf16[16,1024]{1,0:T(8,128)(2,1)} %param.7) | copy-start | bytes 98308
  0.7 17.9 %copy-start.2 = (bf16[2,32,19584]{2,1,0:T(8,128)(2,1)S(1)}, bf16[2,32,19584]{2,1,0:T(8,128)(2,1)}, u32[]{:S(2)}) copy-start(bf16[2,32,19584]{2,1,0:T(8,128)(2,1)} %param.5) | copy-start | bytes 7520260
  18.5 2.0 %copy-start.4 = (s32[32]{0:T(128)S(1)}, s32[32]{0:T(128)}, u32[]{:S(2)}) copy-start(s32[32]{0:T(128)} %param.6) | copy-start | bytes 388
  119.5 4.9 %copy-start = (f32[1024,1024]{1,0:T(8,128)S(1)}, f32[1024,1024]{1,0:T(8,128)}, u32[]{:S(2)}) copy-start(f32[1024,1024]{1,0:T(8,128)} %get-tuple-element.55) | copy-start | bytes 12582916
  119.5 5.9 %copy-start.1 = (f32[1024,1024]{1,0:T(8,128)S(1)}, f32[1024,1024]{1,0:T(8,128)}, u32[]{:S(2)}) copy-start(f32[1024,1024]{1,0:T(8,128)} %get-tuple-element.56) | copy-start | bytes 12582916
  137.6 8.1 %copy-start.5 = (s32[16]{0:T(128)S(1)}, s32[16]{0:T(128)}, u32[]{:S(2)}) copy-start(s32[16]{0:T(128)} %param.8) | copy-start | bytes 196
  155.8 8.1 %all-to-all-start = ((bf16[4,2,512]{2,1,0:T(2,128)(2,1)}), bf16[4,2,512]{2,1,0:T(2,128)(2,1)S(1)}, u32[]{:S(2)}, u32[]{:S(2)}) async-start(bf16[4,2,512]{2,1,0:T(2,128)(2,1)} %reshape.78), calls=%async_computation | async-start | bytes 16384 | tf_op jit(solution)/shard_map/all_to_all | solution.py:71
where the time goes:
time: 189 us; the launch traced here: 187 us
  local copies, waits for them, and re-layouts  123 us (65%)
  other arithmetic  29.3 us (16%)
  blocking collectives  21.6 us (11%)
  matrix products  7.36 us (4%)
  starting transfers between devices  4.24 us (2%)
    gather x96, local copies, waits for them, and re-layouts  85.6 us
    all_gather x1, blocking collectives, on_device(): lax.all_gather(turned, 'elem', axis=3, tiled=True)  21.6 us
    mul x1, other arithmetic, spectra(): jnp.sin(radians) * factor  17.8 us
    unnamed x21, local copies, waits for them, and re-layouts  15.3 us
    reduce_sum x1, other arithmetic, on_device(): jnp.mean(spec_real * spec_real + spec_imag * spec_imag, axis=1)  5.67 us
    slice x1, local copies, waits for them, and re-layouts, spectra(): spec_imag = product[1, :, :, 0] - product[0, :, :, 1]  5.38 us
    convert_element_type x1, other arithmetic, filtered(): return running.astype(jnp.bfloat16)  5.1 us
    dot_general x1, matrix products, spectra(): product = jnp.dot(flattened, basis_high, preferred_element_type=jnp.float32)  4.85 us
  transfers between devices with their start and end apart: 1, of which 1 were waited for; matrix products, arithmetic and copies ran while one was open for 1% of the time, Pallas kernels for 0%

commit v1 on v0

v1 whole, which is shorter than its diff:
```python
import functools
import math

import jax
import jax.numpy as jnp
import numpy as np
from jax import lax
from jax.experimental import pallas as pl
from jax.experimental.pallas import tpu as pltpu
from jax.sharding import PartitionSpec as P

FRAMES = 4
LANES = 128
RADIX = 8
MESH = pl.DeviceIdType.MESH


def fir_kernel(delays_ref, volt_ref, proto_ref, out_ref, seg_ref, coef_ref):
    rows = volt_ref.shape[1]
    taps, chan = proto_ref.shape
    per = chan // LANES
    blocks = FRAMES + taps - 1
    columns = blocks * per
    part, group = pl.program_id(0), pl.program_id(1)

    @pl.when((part == 0) & (group == 0))
    def _():
        for t in range(taps):
            coef_ref[t] = jnp.broadcast_to(
                proto_ref[pl.ds(t, 1), :].astype(jnp.float32), (8, chan)
            )

    lane = lax.broadcasted_iota(jnp.int32, (8, LANES), 1)
    sub = lax.broadcasted_iota(jnp.int32, (8, LANES), 0)
    halves = rows // 8
    index, keep = [], []
    for h in range(halves):
        shift = jnp.zeros((8, LANES), jnp.int32)
        for i in range(8):
            shift = jnp.where(sub == i, delays_ref[group * rows + h * 8 + i], shift)
        index.append((lane + shift) % LANES)
        keep.append(lane < LANES - shift)

    def turned(c):
        both = volt_ref[0, :, pl.ds(c * LANES, LANES)].astype(jnp.float32)
        return [
            jnp.take_along_axis(
                both[8 * h : 8 * h + 8], index[h], axis=1, mode="promise_in_bounds"
            )
            for h in range(halves)
        ]

    now = turned(0)
    for c in range(columns):
        nxt = turned(c + 1)
        for h in range(halves):
            seg_ref[h, :, pl.ds(c * LANES, LANES)] = jnp.where(keep[h], now[h], nxt[h])
        now = nxt
    for j in range(per):
        sums = [[None] * halves for _ in range(FRAMES)]
        for h in range(halves):
            held = [seg_ref[h, :, pl.ds((b * per + j) * LANES, LANES)] for b in range(blocks)]
            for t in range(taps):
                coef = coef_ref[t, :, pl.ds(j * LANES, LANES)]
                for f in range(FRAMES):
                    term = coef * held[f + t]
                    sums[f][h] = term if t == 0 else sums[f][h] + term
        for f in range(FRAMES):
            out_ref[0, f, :, pl.ds(j * LANES, LANES)] = jnp.concatenate(sums[f], axis=0).astype(
                jnp.bfloat16
            )


def fir(delays, voltages, prototype):
    parts, elems, samples = voltages.shape
    taps, chan = prototype.shape
    rows = 16
    window = (FRAMES + taps - 1) * chan
    return pl.pallas_call(
        fir_kernel,
        grid=(parts, elems // rows),
        in_specs=[
            pl.BlockSpec(memory_space=pltpu.SMEM),
            pl.BlockSpec((1, rows, samples), lambda r, g: (r, g, 0)),
            pl.BlockSpec((taps, chan), lambda r, g: (0, 0)),
        ],
        out_specs=pl.BlockSpec((1, FRAMES, rows, chan), lambda r, g: (r, 0, g, 0)),
        out_shape=jax.ShapeDtypeStruct((parts, FRAMES, elems, chan), jnp.bfloat16),
        scratch_shapes=[
            pltpu.VMEM((rows // 8, 8, window), jnp.float32),
            pltpu.VMEM((taps, 8, chan), jnp.float32),
        ],
        compiler_params=pltpu.CompilerParams(
            dimension_semantics=("arbitrary", "arbitrary"), vmem_limit_bytes=24 * 2**20
        ),
    )(delays, voltages, prototype)


def cosine(turns, chan):
    y = jnp.abs(turns % chan - chan // 2) - chan // 4
    x = y.astype(jnp.float32) * (2.0 * math.pi / chan)
    s = x * x
    poly = 1.0 / 362880 - s * (1.0 / 39916800)
    poly = -1.0 / 5040 + s * poly
    poly = 1.0 / 120 + s * poly
    poly = -1.0 / 6 + s * poly
    return (x + x * s * poly) * (chan**-0.5)


def split(value):
    high = value.astype(jnp.bfloat16)
    return high, (value - high.astype(jnp.float32)).astype(jnp.bfloat16)


NT = (((1,), (1,)), ((), ()))


def eight_points(x):
    def add(a, b):
        return (a[0] + b[0], a[1] + b[1])

    def sub(a, b):
        return (a[0] - b[0], a[1] - b[1])

    def minus_i(a):
        return (a[1], -a[0])

    def four(v):
        a, b = add(v[0], v[2]), sub(v[0], v[2])
        c, d = add(v[1], v[3]), minus_i(sub(v[1], v[3]))
        return [add(a, c), add(b, d), sub(a, c), sub(b, d)]

    root = math.sqrt(0.5)
    even = four([add(x[a], x[a + 4]) for a in range(4)])
    d = [sub(x[a], x[a + 4]) for a in range(4)]
    d1 = ((d[1][0] + d[1][1]) * root, (d[1][1] - d[1][0]) * root)
    d3 = ((d[3][1] - d[3][0]) * root, (-d[3][0] - d[3][1]) * root)
    odd = four([d[0], d1, minus_i(d[2]), d3])
    out = []
    for e, o in zip(even, odd):
        out += [e, o]
    return out


def beam_kernel(
    nelem,
    nchan,
    map_ref,
    wave_ref,
    weight_hbm,
    basis_hbm,
    power_ref,
    beam_ref,
    weight_ref,
    basis_ref,
    send_ref,
    recv_ref,
    picked_ref,
    local_sem,
    send_sem,
    recv_sem,
):
    parts, frames, elems, chan = wave_ref.shape
    count = nelem * nchan
    elem_at, chan_at = lax.axis_index("elem"), lax.axis_index("chan")
    me = elem_at * nchan + chan_at
    barrier = pltpu.get_barrier_semaphore()

    def partner(i):
        other = lax.rem(me + i, count)
        return other // nchan, lax.rem(other, nchan)

    def greet(i, carry):
        e, c = partner(i)
        pl.semaphore_signal(barrier, inc=1, device_id=(e, c), device_id_type=MESH)
        return carry

    lax.fori_loop(1, count, greet, 0)
    basis_copy = pltpu.make_async_copy(basis_hbm, basis_ref, local_sem.at[0])
    weight_copy = pltpu.make_async_copy(weight_hbm, weight_ref, local_sem.at[1])
    basis_copy.start()
    weight_copy.start()

    subbands = map_ref.shape[0]
    block = subbands // nchan
    rows = 2 * subbands
    row = lax.broadcasted_iota(jnp.int32, (rows, LANES), 0)
    band = (row // (2 * block)) * block + row % block
    wanted = jnp.zeros((rows, LANES), jnp.int32)
    for s in range(subbands):
        wanted = jnp.where(band == s, map_ref[s], wanted)
    quarter = ((row // block) % 2) * (chan // 4)
    lane = lax.broadcasted_iota(jnp.int32, (rows, LANES), 1)
    real_basis, imag_basis = [], []
    for j in range(chan // LANES):
        turns = wanted * (lane + j * LANES) + quarter
        real_basis.append(cosine(turns, chan))
        imag_basis.append(cosine(turns + 3 * (chan // 4), chan))
    real_basis = split(jnp.concatenate(real_basis, axis=1))
    imag_basis = split(jnp.concatenate(imag_basis, axis=1))
    wave = [wave_ref[r].reshape(frames * elems, chan) for r in range(2)]
    chosen = jnp.zeros((rows, frames * elems), jnp.float32)
    for r, basis in ((0, real_basis), (1, imag_basis)):
        for piece in basis:
            chosen = chosen + lax.dot_general(
                piece, wave[r], NT, preferred_element_type=jnp.float32
            )
    chosen = chosen.astype(jnp.bfloat16)
    for c in range(nchan):
        send_ref[c] = chosen[2 * block * c : 2 * block * (c + 1)]

    pl.semaphore_wait(barrier, count - 1)

    def send(i, carry):
        e, c = partner(i)
        pltpu.make_async_remote_copy(
            src_ref=send_ref.at[c],
            dst_ref=recv_ref.at[me],
            send_sem=send_sem,
            recv_sem=recv_sem,
            device_id=(e, c),
            device_id_type=MESH,
        ).start()
        return carry

    lax.fori_loop(1, count, send, 0)
    recv_ref[me] = send_ref[chan_at]

    lanes = chan // RADIX
    split_wave = [
        tuple(wave[r][:, a * lanes : (a + 1) * lanes].astype(jnp.float32) for r in range(2))
        for a in range(RADIX)
    ]
    classes = eight_points(split_wave)
    basis_copy.wait()
    powers = []
    for c in range(RADIX):
        mixed = jnp.concatenate(classes[c], axis=1).astype(jnp.bfloat16)
        spec = jnp.dot(mixed, basis_ref[c], preferred_element_type=jnp.float32)
        both = spec[:, :lanes] * spec[:, :lanes] + spec[:, lanes:] * spec[:, lanes:]
        total = both[:elems]
        for f in range(1, frames):
            total = total + both[f * elems : (f + 1) * elems]
        powers.append(total * (1.0 / frames))
    wide = lanes // RADIX
    at = lax.broadcasted_iota(jnp.int32, (elems, lanes), 1)
    mixed = []
    for e in range(RADIX):
        piece = None
        for c in range(RADIX):
            shift = (wide * (c - e)) % lanes
            moved = pltpu.roll(powers[c], shift, 1) if shift else powers[c]
            piece = moved if piece is None else jnp.where(at // wide == c, moved, piece)
        mixed.append(piece)
    mixed = jnp.concatenate(mixed, axis=0).astype(jnp.bfloat16)
    down = lax.broadcasted_iota(jnp.int32, (lanes, lanes), 0)
    over = lax.broadcasted_iota(jnp.int32, (lanes, lanes), 1)
    order = (over == (down % wide) * RADIX + down // wide).astype(jnp.float32)
    final = jnp.dot(mixed, order.astype(jnp.bfloat16), preferred_element_type=jnp.float32)
    for e in range(RADIX):
        power_ref[:, e * lanes : (e + 1) * lanes] = final[e * elems : (e + 1) * elems].astype(
            jnp.bfloat16
        )

    weight_rows = weight_ref.shape[0]
    beams = weight_rows // (2 * block)
    down = lax.broadcasted_iota(jnp.int32, (weight_rows, 2 * beams), 0)
    over = lax.broadcasted_iota(jnp.int32, (weight_rows, 2 * beams), 1)
    gather = (down // (2 * block) == over % beams) & ((down // block) % 2 == over // beams)
    gather = gather.astype(jnp.float32).astype(jnp.bfloat16)
    weight_copy.wait()

    arrived = recv_ref.at[pl.ds(0, count - 1)]
    pltpu.make_async_copy(arrived, arrived, recv_sem).wait()

    group = LANES // elems
    inside = lax.broadcasted_iota(jnp.int32, (2 * block, LANES), 1) // elems

    def place(q, carry):
        tiles = [recv_ref[q * group + i].astype(jnp.float32) for i in range(group)]
        pieces = []
        for f in range(frames):
            piece = None
            for i in range(group):
                shift = (elems * (i - f)) % LANES
                moved = pltpu.roll(tiles[i], shift, 1) if shift else tiles[i]
                piece = moved if piece is None else jnp.where(inside == i, moved, piece)
            pieces.append(piece)
        where = pl.multiple_of(q * LANES, LANES)
        picked_ref[:, pl.ds(where, LANES)] = jnp.concatenate(pieces, axis=0).astype(jnp.bfloat16)
        return carry

    steps = count // group
    if steps <= 8:
        for q in range(steps):
            place(q, 0)
    else:
        lax.fori_loop(0, steps, place, 0)
    product = lax.dot_general(
        picked_ref[...], weight_ref[...], NT, preferred_element_type=jnp.float32
    )
    at = lax.broadcasted_iota(jnp.int32, product.shape, 1)
    row = lax.broadcasted_iota(jnp.int32, product.shape, 0)
    product = jnp.where(at % block == row % block, product, 0.0)
    high, low = split(product)
    summed = jnp.dot(high, gather, preferred_element_type=jnp.float32) + jnp.dot(
        low, gather, preferred_element_type=jnp.float32
    )
    for f in range(frames):
        top = summed[2 * block * f : 2 * block * f + block]
        bottom = summed[2 * block * f + block : 2 * block * (f + 1)]
        real = top[:, :beams] - bottom[:, beams:]
        imag = bottom[:, :beams] + top[:, beams:]
        for s in range(block):
            beam_ref[0, pl.ds(s * frames + f, 1), :] = real[s : s + 1]
            beam_ref[1, pl.ds(s * frames + f, 1), :] = imag[s : s + 1]

    pltpu.make_async_copy(arrived, arrived, send_sem).wait()


def class_basis(chan):
    lanes = chan // RADIX
    b = np.arange(lanes)[:, None]
    d = np.arange(lanes)[None, :]
    out = []
    for c in range(RADIX):
        angle = 2.0 * np.pi / chan * (b * (c + RADIX * d) % chan)
        cos, sin = np.cos(angle) * chan**-0.5, np.sin(angle) * chan**-0.5
        out.append(np.block([[cos, -sin], [sin, cos]]))
    return jnp.asarray(np.stack(out), jnp.bfloat16)


def on_device(nelem, nchan, voltages, delays, prototype, subband_map, beam_weights):
    wave = fir(delays, voltages, prototype)
    parts, frames, elems, chan = wave.shape
    beams, _, block, total = beam_weights.shape
    weights = beam_weights.reshape(beams * 2 * block, total)
    basis = class_basis(chan)
    count = nelem * nchan
    return pl.pallas_call(
        functools.partial(beam_kernel, nelem, nchan),
        in_specs=[
            pl.BlockSpec(memory_space=pltpu.SMEM),
            pl.BlockSpec(memory_space=pltpu.VMEM),
            pl.BlockSpec(memory_space=pl.ANY),
            pl.BlockSpec(memory_space=pl.ANY),
        ],
        out_specs=[pl.BlockSpec(memory_space=pltpu.VMEM)] * 2,
        out_shape=[
            jax.ShapeDtypeStruct((elems, chan), jnp.bfloat16),
            jax.ShapeDtypeStruct((2, block * frames, beams), jnp.float32),
        ],
        scratch_shapes=[
            pltpu.VMEM(weights.shape, jnp.bfloat16),
            pltpu.VMEM(basis.shape, jnp.bfloat16),
            pltpu.VMEM((nchan, 2 * block, frames * elems), jnp.bfloat16),
            pltpu.VMEM((count, 2 * block, frames * elems), jnp.bfloat16),
            pltpu.VMEM((2 * block * frames, total), jnp.bfloat16),
            pltpu.SemaphoreType.DMA((2,)),
            pltpu.SemaphoreType.DMA,
            pltpu.SemaphoreType.DMA,
        ],
        compiler_params=pltpu.CompilerParams(collective_id=0, has_side_effects=True),
    )(subband_map, wave, weights, basis)


def solution(mesh):
    return jax.shard_map(
        functools.partial(on_device, mesh.shape["elem"], mesh.shape["chan"]),
        mesh=mesh,
        in_specs=(
            P(None, ("elem", "chan"), None),
            P(("elem", "chan")),
            P(),
            P(),
            P("elem", None, "chan", None),
        ),
        out_specs=(P(("elem", "chan"), None), P(None, "chan", "elem")),
        check_vma=False,
    )
```

time: 189 us -> 24 us (0.13)
  local copies, waits for them, and re-layouts: 123 us -> 7.81 us
  other arithmetic: 29.3 us -> 0 us
  blocking collectives: 21.6 us -> 0 us
  Pallas kernels: 0 us -> 15.2 us
  matrix products: 7.36 us -> 0 us
  starting transfers between devices: 4.24 us -> 0 us
    gather x99 -> x0, local copies, waits for them, and re-layouts: 92.9 us -> none
    all_gather x1 -> x0, blocking collectives: 21.6 us -> none  [on_device(): lax.all_gather(turned, 'elem', axis=3, tiled=True)]
    mul x1 -> x0, other arithmetic: 17.8 us -> none  [spectra(): jnp.sin(radians) * factor]
    pallas_call x0 -> x2, Pallas kernels: none -> 15.2 us  [the longest x1 12.4 us: on_device(): pl.pallas_call(functools.partial(beam_kernel, nelem, nchan), in_specs=[pl...]
    unnamed x21 -> x12, local copies, waits for them, and re-layouts: 15.3 us -> 6.71 us
    dot_general x6 -> x0, matrix products: 7.36 us -> none  [the longest x1 4.85 us: spectra(): product = jnp.dot(flattened, basis_high, preferred_element_type=jnp.float32)]
    slice x3 -> x0, local copies, waits for them, and re-layouts: 6.99 us -> none  [the longest x1 5.38 us: spectra(): spec_imag = product[1, :, :, 0] - product[0, :, :, 1]]
    reshape x3 -> x1, local copies, waits for them, and re-layouts: 7.28 us -> 1.1 us  [on_device(): weights = beam_weights.reshape(beams * 2 * block, total)]
  transfers between devices with their start and end apart: 1 -> 0, of which waited for: 1 -> 0; matrix products, arithmetic and copies ran while one was open for 1% -> 0% of each run, Pallas kernels for 0% -> 0%
where the time goes in v1:
time: 24 us; the launch traced here: 23.7 us
  Pallas kernels  15.2 us (63%)
  local copies, waits for them, and re-layouts  7.81 us (33%)
  between operations  0.67 us (3%)
    pallas_call x1, Pallas kernels, on_device(): pl.pallas_call(functools.partial(beam_kernel, nelem, nchan), in_specs=[pl...  12.4 us
    unnamed x12, local copies, waits for them, and re-layouts  6.71 us
    pallas_call x1, Pallas kernels, fir(): pl.pallas_call(fir_kernel, grid=(parts, elems // rows), in_specs=[pl.Bloc...  2.86 us
    reshape x1, local copies, waits for them, and re-layouts, on_device(): weights = beam_weights.reshape(beams * 2 * block, total)  1.1 us

profile of v1, /device:TPU:0, one launch (start us, length us, event | category | flops | bytes accessed | tf_op | source)
XLA Modules:
  0.0 23.7 jit_solution(9845020066757635160)
XLA Ops:
  0.6 0.0 copy-start
  0.6 1.7 %copy-done = bf16[2,32,19584]{2,1,0:T(8,128)(2,1)S(1)} copy-done((bf16[2,32,19584]{2,1,0:T(8,128)(2,1)S(1)}, bf16[2,32,19584]{2,1,0:T(8,128)(2,1)}, u32[]{:S(2)}) %copy-start) | copy-done | bytes 2506776
  2.3 0.0 copy-start.2
  2.3 0.8 %copy-done.2 = bf16[16,1024]{1,0:T(8,128)(2,1)S(1)} copy-done((bf16[16,1024]{1,0:T(8,128)(2,1)S(1)}, bf16[16,1024]{1,0:T(8,128)(2,1)}, u32[]{:S(2)}) %copy-start.2) | copy-done | bytes 32792
  3.1 0.0 copy-start.3
  3.1 0.7 %copy-done.3 = s32[32]{0:T(128)S(1)} copy-done((s32[32]{0:T(128)S(1)}, s32[32]{0:T(128)}, u32[]{:S(2)}) %copy-start.3) | copy-done | bytes 152
  3.8 0.0 copy-start.4
  3.8 2.9 %shard_map.77.wave_ref = bf16[2,4,32,1024]{3,2,1,0:T(8,128)(2,1)S(1)} custom-call(s32[32]{0:T(128)S(1)} %copy-done.3, bf16[2,32,19584]{2,1,0:T(8,128)(2,1)S(1)} %copy-done, bf16[16,1024]{1,0:T(8,128)(2,1)S(1)} %copy-done.2), custom_call_target="tpu_custom_call" | custom-call | tf_op jit(solution)/shard_map/pallas_call | solution.py:79
  6.6 0.0 copy-start.1
  6.6 0.8 %copy-done.1 = bf16[2,4,32,1024]{3,2,1,0:T(8,128)(2,1)} copy-done((bf16[2,4,32,1024]{3,2,1,0:T(8,128)(2,1)}, bf16[2,4,32,1024]{3,2,1,0:T(8,128)(2,1)S(1)}, u32[]{:S(2)}) %copy-start.1) | copy-done | bytes 524312
  7.4 0.0 copy-done.4
  7.4 1.1 %reshape.7.weight_hbm = bf16[512,1024]{1,0:T(8,128)(2,1)} reshape(bf16[64,2,4,1024]{3,2,1,0:T(4,128)(2,1)S(1)} %copy-done.4) | data formatting | bytes 2097152 | tf_op jit(solution)/shard_map/reshape | solution.py:337
  8.5 12.4 %shard_map.78 = (bf16[32,1024]{1,0:T(8,128)(2,1)}, f32[2,16,64]{2,1,0:T(8,128)}) custom-call(s32[16]{0:T(128)} %map_ref.1, bf16[2,4,32,1024]{3,2,1,0:T(8,128)(2,1)} %copy-done.1, bf16[512,1024]{1,0:T(8,128)(2,1)} %reshape.7.weight_hbm, bf16[8,256,256]{2,1,0:T(8,128)(2,1)} %constant.2.clone.basis_hbm), custom_call_target="tpu_custom_call" | custom-call | tf_op jit(solution)/shard_map/pallas_call | solution.py:340
  20.9 1.5 %copy.10 = bf16[32,1024]{1,0:T(8,128)(2,1)} copy(bf16[32,1024]{1,0:T(8,128)(2,1)} %get-tuple-element.4) | data formatting | bytes 131072
  22.4 1.3 %copy.11 = f32[2,16,64]{2,1,0:T(8,128)} copy(f32[2,16,64]{2,1,0:T(8,128)} %get-tuple-element.5) | data formatting | bytes 16384
Async XLA Ops:
  0.6 1.7 %copy-start = (bf16[2,32,19584]{2,1,0:T(8,128)(2,1)S(1)}, bf16[2,32,19584]{2,1,0:T(8,128)(2,1)}, u32[]{:S(2)}) copy-start(bf16[2,32,19584]{2,1,0:T(8,128)(2,1)} %volt_ref.1) | copy-start | bytes 7520260
  2.3 0.8 %copy-start.2 = (bf16[16,1024]{1,0:T(8,128)(2,1)S(1)}, bf16[16,1024]{1,0:T(8,128)(2,1)}, u32[]{:S(2)}) copy-start(bf16[16,1024]{1,0:T(8,128)(2,1)} %proto_ref.1) | copy-start | bytes 98308
  3.1 0.7 %copy-start.3 = (s32[32]{0:T(128)S(1)}, s32[32]{0:T(128)}, u32[]{:S(2)}) copy-start(s32[32]{0:T(128)} %delays_ref.1) | copy-start | bytes 388
  3.8 3.7 %copy-start.4 = (bf16[64,2,4,1024]{3,2,1,0:T(4,128)(2,1)S(1)}, bf16[64,2,4,1024]{3,2,1,0:T(4,128)(2,1)}, u32[]{:S(2)}) copy-start(bf16[64,2,4,1024]{3,2,1,0:T(4,128)(2,1)} %param.10) | copy-start | bytes 3145732
  6.6 0.8 %copy-start.1 = (bf16[2,4,32,1024]{3,2,1,0:T(8,128)(2,1)}, bf16[2,4,32,1024]{3,2,1,0:T(8,128)(2,1)S(1)}, u32[]{:S(2)}) copy-start(bf16[2,4,32,1024]{3,2,1,0:T(8,128)(2,1)S(1)} %shard_map.77.wave_ref) | copy-start | bytes 1572868

commit v2 on v1

--- a/solution.py
+++ b/solution.py
@@ -15,21 +15,58 @@
 MESH = pl.DeviceIdType.MESH
 
 
-def fir_kernel(delays_ref, volt_ref, proto_ref, out_ref, seg_ref, coef_ref):
+def cosine(turns, chan):
+    y = jnp.abs(turns % chan - chan // 2) - chan // 4
+    x = y.astype(jnp.float32) * (2.0 * math.pi / chan)
+    s = x * x
+    poly = 1.0 / 362880 - s * (1.0 / 39916800)
+    poly = -1.0 / 5040 + s * poly
+    poly = 1.0 / 120 + s * poly
+    poly = -1.0 / 6 + s * poly
+    return (x + x * s * poly) * (chan**-0.5)
+
+
+def split(value):
+    high = value.astype(jnp.bfloat16)
+    return high, (value - high.astype(jnp.float32)).astype(jnp.bfloat16)
+
+
+NT = (((1,), (1,)), ((), ()))
+
+
+def eight_points(x):
+    def add(a, b):
+        return (a[0] + b[0], a[1] + b[1])
+
+    def sub(a, b):
+        return (a[0] - b[0], a[1] - b[1])
+
+    def minus_i(a):
+        return (a[1], -a[0])
+
+    def four(v):
+        a, b = add(v[0], v[2]), sub(v[0], v[2])
+        c, d = add(v[1], v[3]), minus_i(sub(v[1], v[3]))
+        return [add(a, c), add(b, d), sub(a, c), sub(b, d)]
+
+    root = math.sqrt(0.5)
+    even = four([add(x[a], x[a + 4]) for a in range(4)])
+    d = [sub(x[a], x[a + 4]) for a in range(4)]
+    d1 = ((d[1][0] + d[1][1]) * root, (d[1][1] - d[1][0]) * root)
+    d3 = ((d[3][1] - d[3][0]) * root, (-d[3][0] - d[3][1]) * root)
+    odd = four([d[0], d1, minus_i(d[2]), d3])
+    out = []
+    for e, o in zip(even, odd):
+        out += [e, o]
+    return out
+
+
+def filter_chunk(chunk, groups, volt_ref, delay_ref, coef_ref, seg_ref, wave_ref):
     rows = volt_ref.shape[1]
-    taps, chan = proto_ref.shape
+    taps, _, chan = coef_ref.shape
     per = chan // LANES
     blocks = FRAMES + taps - 1
-    columns = blocks * per
-    part, group = pl.program_id(0), pl.program_id(1)
-
-    @pl.when((part == 0) & (group == 0))
-    def _():
-        for t in range(taps):
-            coef_ref[t] = jnp.broadcast_to(
-                proto_ref[pl.ds(t, 1), :].astype(jnp.float32), (8, chan)
-            )
-
+    part, group = chunk // groups, lax.rem(chunk, groups)
     lane = lax.broadcasted_iota(jnp.int32, (8, LANES), 1)
     sub = lax.broadcasted_iota(jnp.int32, (8, LANES), 0)
     halves = rows // 8
@@ -37,12 +74,12 @@
     for h in range(halves):
         shift = jnp.zeros((8, LANES), jnp.int32)
         for i in range(8):
-            shift = jnp.where(sub == i, delays_ref[group * rows + h * 8 + i], shift)
+            shift = jnp.where(sub == i, delay_ref[group * rows + h * 8 + i], shift)
         index.append((lane + shift) % LANES)
         keep.append(lane < LANES - shift)
 
     def turned(c):
-        both = volt_ref[0, :, pl.ds(c * LANES, LANES)].astype(jnp.float32)
+        both = volt_ref[chunk, :, pl.ds(c * LANES, LANES)].astype(jnp.float32)
         return [
             jnp.take_along_axis(
                 both[8 * h : 8 * h + 8], index[h], axis=1, mode="promise_in_bounds"
@@ -51,11 +88,12 @@
         ]
 
     now = turned(0)
-    for c in range(columns):
+    for c in range(blocks * per):
         nxt = turned(c + 1)
         for h in range(halves):
             seg_ref[h, :, pl.ds(c * LANES, LANES)] = jnp.where(keep[h], now[h], nxt[h])
         now = nxt
+    where = pl.multiple_of(group * rows, rows)
     for j in range(per):
         sums = [[None] * halves for _ in range(FRAMES)]
         for h in range(halves):
@@ -66,101 +104,44 @@
                     term = coef * held[f + t]
                     sums[f][h] = term if t == 0 else sums[f][h] + term
         for f in range(FRAMES):
-            out_ref[0, f, :, pl.ds(j * LANES, LANES)] = jnp.concatenate(sums[f], axis=0).astype(
-                jnp.bfloat16
-            )
-
-
-def fir(delays, voltages, prototype):
-    parts, elems, samples = voltages.shape
-    taps, chan = prototype.shape
-    rows = 16
-    window = (FRAMES + taps - 1) * chan
-    return pl.pallas_call(
-        fir_kernel,
-        grid=(parts, elems // rows),
-        in_specs=[
-            pl.BlockSpec(memory_space=pltpu.SMEM),
-            pl.BlockSpec((1, rows, samples), lambda r, g: (r, g, 0)),
-            pl.BlockSpec((taps, chan), lambda r, g: (0, 0)),
-        ],
-        out_specs=pl.BlockSpec((1, FRAMES, rows, chan), lambda r, g: (r, 0, g, 0)),
-        out_shape=jax.ShapeDtypeStruct((parts, FRAMES, elems, chan), jnp.bfloat16),
-        scratch_shapes=[
-            pltpu.VMEM((rows // 8, 8, window), jnp.float32),
-            pltpu.VMEM((taps, 8, chan), jnp.float32),
-        ],
-        compiler_params=pltpu.CompilerParams(
-            dimension_semantics=("arbitrary", "arbitrary"), vmem_limit_bytes=24 * 2**20
-        ),
-    )(delays, voltages, prototype)
-
-
-def cosine(turns, chan):
-    y = jnp.abs(turns % chan - chan // 2) - chan // 4
-    x = y.astype(jnp.float32) * (2.0 * math.pi / chan)
-    s = x * x
-    poly = 1.0 / 362880 - s * (1.0 / 39916800)
-    poly = -1.0 / 5040 + s * poly
-    poly = 1.0 / 120 + s * poly
-    poly = -1.0 / 6 + s * poly
-    return (x + x * s * poly) * (chan**-0.5)
-
-
-def split(value):
-    high = value.astype(jnp.bfloat16)
-    return high, (value - high.astype(jnp.float32)).astype(jnp.bfloat16)
-
-
-NT = (((1,), (1,)), ((), ()))
-
-
-def eight_points(x):
-    def add(a, b):
-        return (a[0] + b[0], a[1] + b[1])
-
-    def sub(a, b):
-        return (a[0] - b[0], a[1] - b[1])
-
-    def minus_i(a):
-        return (a[1], -a[0])
-
-    def four(v):
-        a, b = add(v[0], v[2]), sub(v[0], v[2])
-        c, d = add(v[1], v[3]), minus_i(sub(v[1], v[3]))
-        return [add(a, c), add(b, d), sub(a, c), sub(b, d)]
-
-    root = math.sqrt(0.5)
-    even = four([add(x[a], x[a + 4]) for a in range(4)])
-    d = [sub(x[a], x[a + 4]) for a in range(4)]
-    d1 = ((d[1][0] + d[1][1]) * root, (d[1][1] - d[1][0]) * root)
-    d3 = ((d[3][1] - d[3][0]) * root, (-d[3][0] - d[3][1]) * root)
-    odd = four([d[0], d1, minus_i(d[2]), d3])
-    out = []
-    for e, o in zip(even, odd):
-        out += [e, o]
-    return out
-
-
-def beam_kernel(
+            wave_ref[part, f, pl.ds(where, rows), pl.ds(j * LANES, LANES)] = jnp.concatenate(
+                sums[f], axis=0
+            ).astype(jnp.bfloat16)
+
+
+def main_kernel(
     nelem,
     nchan,
-    map_ref,
-    wave_ref,
+    delay_hbm,
+    map_hbm,
+    volt_hbm,
+    proto_hbm,
     weight_hbm,
     basis_hbm,
     power_ref,
     beam_ref,
+    delay_ref,
+    map_ref,
+    volt_ref,
+    proto_ref,
+    raw_ref,
+    basis_ref,
+    seg_ref,
+    coef_ref,
+    wave_ref,
     weight_ref,
-    basis_ref,
     send_ref,
     recv_ref,
     picked_ref,
     local_sem,
+    volt_sem,
     send_sem,
     recv_sem,
 ):
     parts, frames, elems, chan = wave_ref.shape
+    chunks, chunk_rows, _ = volt_ref.shape
+    groups = chunks // parts
+    taps = proto_ref.shape[0]
     count = nelem * nchan
     elem_at, chan_at = lax.axis_index("elem"), lax.axis_index("chan")
     me = elem_at * nchan + chan_at
@@ -170,16 +151,34 @@
         other = lax.rem(me + i, count)
         return other // nchan, lax.rem(other, nchan)
 
+    map_copy = pltpu.make_async_copy(map_hbm, map_ref, local_sem.at[0])
+    proto_copy = pltpu.make_async_copy(proto_hbm, proto_ref, local_sem.at[1])
+    delay_copy = pltpu.make_async_copy(delay_hbm, delay_ref, local_sem.at[2])
+    basis_copy = pltpu.make_async_copy(basis_hbm, basis_ref, local_sem.at[3])
+    weight_copy = pltpu.make_async_copy(weight_hbm, raw_ref, local_sem.at[4])
+    volt_copies = [
+        pltpu.make_async_copy(
+            volt_hbm.at[k // groups, pl.ds(k % groups * chunk_rows, chunk_rows)],
+            volt_ref.at[k],
+            volt_sem.at[k],
+        )
+        for k in range(chunks)
+    ]
+    map_copy.start()
+    proto_copy.start()
+    delay_copy.start()
+    for copy in volt_copies:
+        copy.start()
+    basis_copy.start()
+    weight_copy.start()
+
     def greet(i, carry):
         e, c = partner(i)
         pl.semaphore_signal(barrier, inc=1, device_id=(e, c), device_id_type=MESH)
         return carry
 
     lax.fori_loop(1, count, greet, 0)
-    basis_copy = pltpu.make_async_copy(basis_hbm, basis_ref, local_sem.at[0])
-    weight_copy = pltpu.make_async_copy(weight_hbm, weight_ref, local_sem.at[1])
-    basis_copy.start()
-    weight_copy.start()
+    map_copy.wait()
 
     subbands = map_ref.shape[0]
     block = subbands // nchan
@@ -198,6 +197,21 @@
         imag_basis.append(cosine(turns + 3 * (chan // 4), chan))
     real_basis = split(jnp.concatenate(real_basis, axis=1))
     imag_basis = split(jnp.concatenate(imag_basis, axis=1))
+    proto_copy.wait()
+    for t in range(taps):
+        coef_ref[t] = jnp.broadcast_to(
+            proto_ref[pl.ds(t, 1), :].astype(jnp.float32), (8, chan)
+        )
+    delay_copy.wait()
+
+    def filter_step(k, carry):
+        pltpu.make_async_copy(
+            volt_hbm.at[0, pl.ds(0, chunk_rows)], volt_ref.at[k], volt_sem.at[k]
+        ).wait()
+        filter_chunk(k, groups, volt_ref, delay_ref, coef_ref, seg_ref, wave_ref)
+        return carry
+
+    lax.fori_loop(0, chunks, filter_step, 0)
     wave = [wave_ref[r].reshape(frames * elems, chan) for r in range(2)]
     chosen = jnp.zeros((rows, frames * elems), jnp.float32)
     for r, basis in ((0, real_basis), (1, imag_basis)):
@@ -269,6 +283,10 @@
     gather = (down // (2 * block) == over % beams) & ((down // block) % 2 == over // beams)
     gather = gather.astype(jnp.float32).astype(jnp.bfloat16)
     weight_copy.wait()
+    step = min(8, raw_ref.shape[0])
+    for i in range(0, raw_ref.shape[0], step):
+        piece = raw_ref[i : i + step].reshape(step * 2 * block, raw_ref.shape[3])
+        weight_ref[2 * block * i : 2 * block * (i + step)] = piece
 
     arrived = recv_ref.at[pl.ds(0, count - 1)]
     pltpu.make_async_copy(arrived, arrived, recv_sem).wait()
@@ -330,38 +348,66 @@
     return jnp.asarray(np.stack(out), jnp.bfloat16)
 
 
+def deliver_kernel(power_from, beam_from, power_to, beam_to, sems):
+    copies = [
+        pltpu.make_async_copy(power_from, power_to, sems.at[0]),
+        pltpu.make_async_copy(beam_from, beam_to, sems.at[1]),
+    ]
+    for copy in copies:
+        copy.start()
+    for copy in copies:
+        copy.wait()
+
+
 def on_device(nelem, nchan, voltages, delays, prototype, subband_map, beam_weights):
-    wave = fir(delays, voltages, prototype)
-    parts, frames, elems, chan = wave.shape
+    parts, elems, samples = voltages.shape
+    taps, chan = prototype.shape
     beams, _, block, total = beam_weights.shape
-    weights = beam_weights.reshape(beams * 2 * block, total)
+    window = (FRAMES + taps - 1) * chan
     basis = class_basis(chan)
     count = nelem * nchan
-    return pl.pallas_call(
-        functools.partial(beam_kernel, nelem, nchan),
-        in_specs=[
-            pl.BlockSpec(memory_space=pltpu.SMEM),
-            pl.BlockSpec(memory_space=pltpu.VMEM),
-            pl.BlockSpec(memory_space=pl.ANY),
-            pl.BlockSpec(memory_space=pl.ANY),
-        ],
+    rows = 16
+    chunks = parts * elems // rows
+    out_shape = [
+        jax.ShapeDtypeStruct((elems, chan), jnp.bfloat16),
+        jax.ShapeDtypeStruct((2, block * FRAMES, beams), jnp.float32),
+    ]
+    power, beam = pl.pallas_call(
+        functools.partial(main_kernel, nelem, nchan),
+        in_specs=[pl.BlockSpec(memory_space=pltpu.HBM)] * 6,
         out_specs=[pl.BlockSpec(memory_space=pltpu.VMEM)] * 2,
-        out_shape=[
-            jax.ShapeDtypeStruct((elems, chan), jnp.bfloat16),
-            jax.ShapeDtypeStruct((2, block * frames, beams), jnp.float32),
-        ],
+        out_shape=[pltpu.VMEM(o.shape, o.dtype) for o in out_shape],
         scratch_shapes=[
-            pltpu.VMEM(weights.shape, jnp.bfloat16),
+            pltpu.SMEM(delays.shape, jnp.int32),
+            pltpu.SMEM(subband_map.shape, jnp.int32),
+            pltpu.VMEM((chunks, rows, samples), jnp.bfloat16),
+            pltpu.VMEM((taps, chan), jnp.bfloat16),
+            pltpu.VMEM(beam_weights.shape, jnp.bfloat16),
             pltpu.VMEM(basis.shape, jnp.bfloat16),
-            pltpu.VMEM((nchan, 2 * block, frames * elems), jnp.bfloat16),
-            pltpu.VMEM((count, 2 * block, frames * elems), jnp.bfloat16),
-            pltpu.VMEM((2 * block * frames, total), jnp.bfloat16),
-            pltpu.SemaphoreType.DMA((2,)),
+            pltpu.VMEM((rows // 8, 8, window), jnp.float32),
+            pltpu.VMEM((taps, 8, chan), jnp.float32),
+            pltpu.VMEM((parts, FRAMES, elems, chan), jnp.bfloat16),
+            pltpu.VMEM((beams * 2 * block, total), jnp.bfloat16),
+            pltpu.VMEM((nchan, 2 * block, FRAMES * elems), jnp.bfloat16),
+            pltpu.VMEM((count, 2 * block, FRAMES * elems), jnp.bfloat16),
+            pltpu.VMEM((2 * block * FRAMES, total), jnp.bfloat16),
+            pltpu.SemaphoreType.DMA((5,)),
+            pltpu.SemaphoreType.DMA((chunks,)),
             pltpu.SemaphoreType.DMA,
             pltpu.SemaphoreType.DMA,
         ],
-        compiler_params=pltpu.CompilerParams(collective_id=0, has_side_effects=True),
-    )(subband_map, wave, weights, basis)
+        compiler_params=pltpu.CompilerParams(
+            collective_id=0, has_side_effects=True, vmem_limit_bytes=66_400_000
+        ),
+    )(delays, subband_map, voltages, prototype, beam_weights, basis)
+    return pl.pallas_call(
+        deliver_kernel,
+        in_specs=[pl.BlockSpec(memory_space=pl.ANY)] * 2,
+        out_specs=[pl.BlockSpec(memory_space=pl.ANY)] * 2,
+        out_shape=out_shape,
+        scratch_shapes=[pltpu.SemaphoreType.DMA((2,))],
+        compiler_params=pltpu.CompilerParams(vmem_limit_bytes=2**20),
+    )(power, beam)
 
 
 def solution(mesh):

time: 24 us -> 14.7 us (0.61)
  local copies, waits for them, and re-layouts: 7.81 us -> 0 us
  Pallas kernels: 15.2 us -> 13.9 us
    unnamed x12 -> x0, local copies, waits for them, and re-layouts: 6.71 us -> none
    pallas_call x2, Pallas kernels: 15.2 us -> 13.9 us  [the longest x1 13.3 us: on_device(): pl.pallas_call(functools.partial(main_kernel, nelem, nchan), in_specs=[pl...]
    reshape x1 -> x0, local copies, waits for them, and re-layouts: 1.1 us -> none  [on_device(): weights = beam_weights.reshape(beams * 2 * block, total)]
where the time goes in v2:
time: 14.7 us; the launch traced here: 14.6 us
  Pallas kernels  13.9 us (95%)
  between operations  0.64 us (4%)
    pallas_call x1, Pallas kernels, on_device(): pl.pallas_call(functools.partial(main_kernel, nelem, nchan), in_specs=[pl...  13.3 us
    pallas_call x1, Pallas kernels, on_device(): pl.pallas_call(deliver_kernel, in_specs=[pl.BlockSpec(memory_space=pl.ANY...  0.65 us

profile of v2, /device:TPU:0, one launch (start us, length us, event | category | flops | bytes accessed | tf_op | source)
XLA Modules:
  0.0 14.6 jit_solution(3621404740807263491)
XLA Ops:
  0.6 13.3 %shard_map.77 = (bf16[32,1024]{1,0:T(8,128)(2,1)S(1)}, f32[2,16,64]{2,1,0:T(8,128)S(1)}) custom-call(s32[32]{0:T(128)} %delay_hbm.1, s32[16]{0:T(128)} %map_hbm.1, bf16[2,32,19584]{2,1,0:T(8,128)(2,1)} %volt_hbm.1, bf16[16,1024]{1,0:T(8,128)(2,1)} %proto_hbm.1, bf16[64,2,4,1024]{3,2,1,0:T(4,128)(2,1)} %weight_hbm.1, bf16[8,256,256]{2,1,0:T(8,128)(2,1)} %constant.2.clone.basis_hbm), custom_call_target="tpu_custom_call" | custom-call | tf_op jit(solution)/shard_map/pallas_call | solution.py:375
  13.9 0.7 %shard_map.78 = (bf16[32,1024]{1,0:T(8,128)(2,1)}, f32[2,16,64]{2,1,0:T(8,128)}) custom-call(bf16[32,1024]{1,0:T(8,128)(2,1)S(1)} %get-tuple-element.4.power_from, f32[2,16,64]{2,1,0:T(8,128)S(1)} %get-tuple-element.5.beam_from), custom_call_target="tpu_custom_call" | custom-call | tf_op jit(solution)/shard_map/pallas_call | solution.py:403

commit v3 on v2

--- a/solution.py
+++ b/solution.py
@@ -12,7 +12,7 @@
 FRAMES = 4
 LANES = 128
 RADIX = 8
-MESH = pl.DeviceIdType.MESH
+LOGICAL = pl.DeviceIdType.LOGICAL
 
 
 def cosine(turns, chan):
@@ -148,8 +148,8 @@
     barrier = pltpu.get_barrier_semaphore()
 
     def partner(i):
-        other = lax.rem(me + i, count)
-        return other // nchan, lax.rem(other, nchan)
+        other = me + i
+        return jnp.where(other >= count, other - count, other)
 
     map_copy = pltpu.make_async_copy(map_hbm, map_ref, local_sem.at[0])
     proto_copy = pltpu.make_async_copy(proto_hbm, proto_ref, local_sem.at[1])
@@ -169,15 +169,16 @@
     delay_copy.start()
     for copy in volt_copies:
         copy.start()
-    basis_copy.start()
-    weight_copy.start()
 
     def greet(i, carry):
-        e, c = partner(i)
-        pl.semaphore_signal(barrier, inc=1, device_id=(e, c), device_id_type=MESH)
+        pl.semaphore_signal(barrier, inc=1, device_id=partner(i), device_id_type=LOGICAL)
         return carry
 
-    lax.fori_loop(1, count, greet, 0)
+    if count <= 64:
+        for i in sorted(range(1, count), key=lambda i: -min(i, count - i)):
+            greet(i, 0)
+    else:
+        lax.fori_loop(1, count, greet, 0)
     map_copy.wait()
 
     subbands = map_ref.shape[0]
@@ -208,6 +209,12 @@
         pltpu.make_async_copy(
             volt_hbm.at[0, pl.ds(0, chunk_rows)], volt_ref.at[k], volt_sem.at[k]
         ).wait()
+
+        @pl.when(k == chunks - 1)
+        def _():
+            basis_copy.start()
+            weight_copy.start()
+
         filter_chunk(k, groups, volt_ref, delay_ref, coef_ref, seg_ref, wave_ref)
         return carry
 
@@ -226,18 +233,22 @@
     pl.semaphore_wait(barrier, count - 1)
 
     def send(i, carry):
-        e, c = partner(i)
+        other = partner(i)
         pltpu.make_async_remote_copy(
-            src_ref=send_ref.at[c],
+            src_ref=send_ref.at[lax.rem(other, nchan)],
             dst_ref=recv_ref.at[me],
             send_sem=send_sem,
             recv_sem=recv_sem,
-            device_id=(e, c),
-            device_id_type=MESH,
+            device_id=other,
+            device_id_type=LOGICAL,
         ).start()
         return carry
 
-    lax.fori_loop(1, count, send, 0)
+    if count <= 64:
+        for i in sorted(range(1, count), key=lambda i: -min(i, count - i)):
+            send(i, 0)
+    else:
+        lax.fori_loop(1, count, send, 0)
     recv_ref[me] = send_ref[chan_at]
 
     lanes = chan // RADIX

time: 14.7 us -> 15.4 us (1.048)
  Pallas kernels: 13.9 us -> 14.6 us
    pallas_call x1, Pallas kernels: 13.3 us -> 13.9 us  [on_device(): pl.pallas_call(functools.partial(main_kernel, nelem, nchan), in_specs=[pl...]
where the time goes in v3:
time: 15.4 us; the launch traced here: 15.2 us
  Pallas kernels  14.6 us (95%)
  between operations  0.64 us (4%)
    pallas_call x1, Pallas kernels, on_device(): pl.pallas_call(functools.partial(main_kernel, nelem, nchan), in_specs=[pl...  13.9 us
    pallas_call x1, Pallas kernels, on_device(): pl.pallas_call(deliver_kernel, in_specs=[pl.BlockSpec(memory_space=pl.ANY...  0.65 us

profile of v3, /device:TPU:0, one launch (start us, length us, event | category | flops | bytes accessed | tf_op | source)
XLA Modules:
  0.0 15.2 jit_solution(5312690722433343677)
XLA Ops:
  0.6 13.9 %shard_map.77 = (bf16[32,1024]{1,0:T(8,128)(2,1)S(1)}, f32[2,16,64]{2,1,0:T(8,128)S(1)}) custom-call(s32[32]{0:T(128)} %delay_hbm.1, s32[16]{0:T(128)} %map_hbm.1, bf16[2,32,19584]{2,1,0:T(8,128)(2,1)} %volt_hbm.1, bf16[16,1024]{1,0:T(8,128)(2,1)} %proto_hbm.1, bf16[64,2,4,1024]{3,2,1,0:T(4,128)(2,1)} %weight_hbm.1, bf16[8,256,256]{2,1,0:T(8,128)(2,1)} %constant.2.clone.basis_hbm), custom_call_target="tpu_custom_call" | custom-call | tf_op jit(solution)/shard_map/pallas_call | solution.py:386
  14.6 0.7 %shard_map.78 = (bf16[32,1024]{1,0:T(8,128)(2,1)}, f32[2,16,64]{2,1,0:T(8,128)}) custom-call(bf16[32,1024]{1,0:T(8,128)(2,1)S(1)} %get-tuple-element.4.power_from, f32[2,16,64]{2,1,0:T(8,128)S(1)} %get-tuple-element.5.beam_from), custom_call_target="tpu_custom_call" | custom-call | tf_op jit(solution)/shard_map/pallas_call | solution.py:414

commit v4 on v3

--- a/solution.py
+++ b/solution.py
@@ -16,7 +16,7 @@
 
 
 def cosine(turns, chan):
-    y = jnp.abs(turns % chan - chan // 2) - chan // 4
+    y = jnp.abs((turns & (chan - 1)) - chan // 2) - chan // 4
     x = y.astype(jnp.float32) * (2.0 * math.pi / chan)
     s = x * x
     poly = 1.0 / 362880 - s * (1.0 / 39916800)
@@ -75,7 +75,7 @@
         shift = jnp.zeros((8, LANES), jnp.int32)
         for i in range(8):
             shift = jnp.where(sub == i, delay_ref[group * rows + h * 8 + i], shift)
-        index.append((lane + shift) % LANES)
+        index.append((lane + shift) & (LANES - 1))
         keep.append(lane < LANES - shift)
 
     def turned(c):
@@ -147,9 +147,24 @@
     me = elem_at * nchan + chan_at
     barrier = pltpu.get_barrier_semaphore()
 
-    def partner(i):
-        other = me + i
-        return jnp.where(other >= count, other - count, other)
+    def each_partner(act):
+        near_start = elem_at < nelem // 2
+
+        def row(k, carry):
+            first = jnp.where(near_start, nelem - 1 - k, k) * nchan
+            for c in range(nchan):
+
+                @pl.when(first + c != me)
+                def _():
+                    act(first + c, c)
+
+            return carry
+
+        if count <= 64:
+            for k in range(nelem):
+                row(k, 0)
+        else:
+            lax.fori_loop(0, nelem, row, 0)
 
     map_copy = pltpu.make_async_copy(map_hbm, map_ref, local_sem.at[0])
     proto_copy = pltpu.make_async_copy(proto_hbm, proto_ref, local_sem.at[1])
@@ -170,15 +185,10 @@
     for copy in volt_copies:
         copy.start()
 
-    def greet(i, carry):
-        pl.semaphore_signal(barrier, inc=1, device_id=partner(i), device_id_type=LOGICAL)
-        return carry
-
-    if count <= 64:
-        for i in sorted(range(1, count), key=lambda i: -min(i, count - i)):
-            greet(i, 0)
-    else:
-        lax.fori_loop(1, count, greet, 0)
+    def greet(other, c):
+        pl.semaphore_signal(barrier, inc=1, device_id=other, device_id_type=LOGICAL)
+
+    each_partner(greet)
     map_copy.wait()
 
     subbands = map_ref.shape[0]
@@ -232,23 +242,17 @@
 
     pl.semaphore_wait(barrier, count - 1)
 
-    def send(i, carry):
-        other = partner(i)
+    def send(other, c):
         pltpu.make_async_remote_copy(
-            src_ref=send_ref.at[lax.rem(other, nchan)],
+            src_ref=send_ref.at[c],
             dst_ref=recv_ref.at[me],
             send_sem=send_sem,
             recv_sem=recv_sem,
             device_id=other,
             device_id_type=LOGICAL,
         ).start()
-        return carry
-
-    if count <= 64:
-        for i in sorted(range(1, count), key=lambda i: -min(i, count - i)):
-            send(i, 0)
-    else:
-        lax.fori_loop(1, count, send, 0)
+
+    each_partner(send)
     recv_ref[me] = send_ref[chan_at]
 
     lanes = chan // RADIX

time: 15.4 us -> 14.8 us (0.961)
  Pallas kernels: 14.6 us -> 14 us
    pallas_call x1, Pallas kernels: 13.9 us -> 13.4 us  [on_device(): pl.pallas_call(functools.partial(main_kernel, nelem, nchan), in_specs=[pl...]
where the time goes in v4:
time: 14.8 us; the launch traced here: 14.7 us
  Pallas kernels  14 us (95%)
  between operations  0.64 us (4%)
    pallas_call x1, Pallas kernels, on_device(): pl.pallas_call(functools.partial(main_kernel, nelem, nchan), in_specs=[pl...  13.4 us
    pallas_call x1, Pallas kernels, on_device(): pl.pallas_call(deliver_kernel, in_specs=[pl.BlockSpec(memory_space=pl.ANY...  0.65 us

profile of v4, /device:TPU:0, one launch (start us, length us, event | category | flops | bytes accessed | tf_op | source)
XLA Modules:
  0.0 14.7 jit_solution(14962214902615839335)
XLA Ops:
  0.6 13.4 %shard_map.77 = (bf16[32,1024]{1,0:T(8,128)(2,1)S(1)}, f32[2,16,64]{2,1,0:T(8,128)S(1)}) custom-call(s32[32]{0:T(128)} %delay_hbm.1, s32[16]{0:T(128)} %map_hbm.1, bf16[2,32,19584]{2,1,0:T(8,128)(2,1)} %volt_hbm.1, bf16[16,1024]{1,0:T(8,128)(2,1)} %proto_hbm.1, bf16[64,2,4,1024]{3,2,1,0:T(4,128)(2,1)} %weight_hbm.1, bf16[8,256,256]{2,1,0:T(8,128)(2,1)} %constant.2.clone.basis_hbm), custom_call_target="tpu_custom_call" | custom-call | tf_op jit(solution)/shard_map/pallas_call | solution.py:390
  14.0 0.7 %shard_map.78 = (bf16[32,1024]{1,0:T(8,128)(2,1)}, f32[2,16,64]{2,1,0:T(8,128)}) custom-call(bf16[32,1024]{1,0:T(8,128)(2,1)S(1)} %get-tuple-element.4.power_from, f32[2,16,64]{2,1,0:T(8,128)S(1)} %get-tuple-element.5.beam_from), custom_call_target="tpu_custom_call" | custom-call | tf_op jit(solution)/shard_map/pallas_call | solution.py:418

commit v5 on v4

--- a/solution.py
+++ b/solution.py
@@ -61,52 +61,49 @@
     return out
 
 
-def filter_chunk(chunk, groups, volt_ref, delay_ref, coef_ref, seg_ref, wave_ref):
-    rows = volt_ref.shape[1]
+def turn_plan(chunk, groups, rows, delay_ref):
+    lane = lax.broadcasted_iota(jnp.int32, (rows, LANES), 1)
+    sub = lax.broadcasted_iota(jnp.int32, (rows, LANES), 0)
+    shift = jnp.zeros((rows, LANES), jnp.int32)
+    for i in range(rows):
+        shift = jnp.where(sub == i, delay_ref[chunk % groups * rows + i], shift)
+    return (lane + shift) & (LANES - 1), lane < LANES - shift
+
+
+def turn_columns(chunk, first, last, held, plan, volt_ref, seg_ref):
+    index, keep = plan
+
+    def turned(c):
+        value = volt_ref[chunk, :, pl.ds(c * LANES, LANES)].astype(jnp.float32)
+        return jnp.take_along_axis(value, index, axis=1, mode="promise_in_bounds")
+
+    now = turned(first) if held is None else held
+    for c in range(first, last):
+        nxt = turned(c + 1)
+        seg_ref[chunk % 2, :, pl.ds(c * LANES, LANES)] = jnp.where(keep, now, nxt)
+        now = nxt
+    return now
+
+
+def filter_column(chunk, groups, j, coef_ref, seg_ref, wave_ref):
+    rows = seg_ref.shape[1]
     taps, _, chan = coef_ref.shape
     per = chan // LANES
-    blocks = FRAMES + taps - 1
-    part, group = chunk // groups, lax.rem(chunk, groups)
-    lane = lax.broadcasted_iota(jnp.int32, (8, LANES), 1)
-    sub = lax.broadcasted_iota(jnp.int32, (8, LANES), 0)
-    halves = rows // 8
-    index, keep = [], []
-    for h in range(halves):
-        shift = jnp.zeros((8, LANES), jnp.int32)
-        for i in range(8):
-            shift = jnp.where(sub == i, delay_ref[group * rows + h * 8 + i], shift)
-        index.append((lane + shift) & (LANES - 1))
-        keep.append(lane < LANES - shift)
-
-    def turned(c):
-        both = volt_ref[chunk, :, pl.ds(c * LANES, LANES)].astype(jnp.float32)
-        return [
-            jnp.take_along_axis(
-                both[8 * h : 8 * h + 8], index[h], axis=1, mode="promise_in_bounds"
-            )
-            for h in range(halves)
-        ]
-
-    now = turned(0)
-    for c in range(blocks * per):
-        nxt = turned(c + 1)
-        for h in range(halves):
-            seg_ref[h, :, pl.ds(c * LANES, LANES)] = jnp.where(keep[h], now[h], nxt[h])
-        now = nxt
-    where = pl.multiple_of(group * rows, rows)
-    for j in range(per):
-        sums = [[None] * halves for _ in range(FRAMES)]
-        for h in range(halves):
-            held = [seg_ref[h, :, pl.ds((b * per + j) * LANES, LANES)] for b in range(blocks)]
-            for t in range(taps):
-                coef = coef_ref[t, :, pl.ds(j * LANES, LANES)]
-                for f in range(FRAMES):
-                    term = coef * held[f + t]
-                    sums[f][h] = term if t == 0 else sums[f][h] + term
+    part, group = chunk // groups, chunk % groups
+    held = [
+        seg_ref[chunk % 2, :, pl.ds((b * per + j) * LANES, LANES)]
+        for b in range(FRAMES + taps - 1)
+    ]
+    sums = [None] * FRAMES
+    for t in range(taps):
+        coef = coef_ref[t, :, pl.ds(j * LANES, LANES)]
         for f in range(FRAMES):
-            wave_ref[part, f, pl.ds(where, rows), pl.ds(j * LANES, LANES)] = jnp.concatenate(
-                sums[f], axis=0
-            ).astype(jnp.bfloat16)
+            term = coef * held[f + t]
+            sums[f] = term if t == 0 else sums[f] + term
+    for f in range(FRAMES):
+        wave_ref[part, f, pl.ds(group * rows, rows), pl.ds(j * LANES, LANES)] = sums[f].astype(
+            jnp.bfloat16
+        )
 
 
 def main_kernel(
@@ -182,7 +179,8 @@
     map_copy.start()
     proto_copy.start()
     delay_copy.start()
-    for copy in volt_copies:
+    ahead = min(4, chunks)
+    for copy in volt_copies[:ahead]:
         copy.start()
 
     def greet(other, c):
@@ -215,20 +213,32 @@
         )
     delay_copy.wait()
 
-    def filter_step(k, carry):
-        pltpu.make_async_copy(
-            volt_hbm.at[0, pl.ds(0, chunk_rows)], volt_ref.at[k], volt_sem.at[k]
-        ).wait()
-
-        @pl.when(k == chunks - 1)
-        def _():
+    per = chan // LANES
+    step = (frames + taps - 1) * per // per
+
+    def arrive(k):
+        volt_copies[k].wait()
+        if k + ahead < chunks:
+            volt_copies[k + ahead].start()
+        elif k + ahead == chunks:
             basis_copy.start()
             weight_copy.start()
 
-        filter_chunk(k, groups, volt_ref, delay_ref, coef_ref, seg_ref, wave_ref)
-        return carry
-
-    lax.fori_loop(0, chunks, filter_step, 0)
+    arrive(0)
+    plan = turn_plan(0, groups, chunk_rows, delay_ref)
+    turn_columns(0, 0, step * per, None, plan, volt_ref, seg_ref)
+    for k in range(chunks):
+        held = None
+        if k + 1 < chunks:
+            arrive(k + 1)
+            plan = turn_plan(k + 1, groups, chunk_rows, delay_ref)
+        for j in range(per):
+            filter_column(k, groups, j, coef_ref, seg_ref, wave_ref)
+            if k + 1 < chunks:
+                held = turn_columns(
+                    k + 1, j * step, (j + 1) * step, held, plan, volt_ref, seg_ref
+                )
+
     wave = [wave_ref[r].reshape(frames * elems, chan) for r in range(2)]
     chosen = jnp.zeros((rows, frames * elems), jnp.float32)
     for r, basis in ((0, real_basis), (1, imag_basis)):
@@ -381,7 +391,7 @@
     window = (FRAMES + taps - 1) * chan
     basis = class_basis(chan)
     count = nelem * nchan
-    rows = 16
+    rows = 8
     chunks = parts * elems // rows
     out_shape = [
         jax.ShapeDtypeStruct((elems, chan), jnp.bfloat16),
@@ -399,8 +409,8 @@
             pltpu.VMEM((taps, chan), jnp.bfloat16),
             pltpu.VMEM(beam_weights.shape, jnp.bfloat16),
             pltpu.VMEM(basis.shape, jnp.bfloat16),
-            pltpu.VMEM((rows // 8, 8, window), jnp.float32),
-            pltpu.VMEM((taps, 8, chan), jnp.float32),
+            pltpu.VMEM((2, rows, window), jnp.float32),
+            pltpu.VMEM((taps, rows, chan), jnp.float32),
             pltpu.VMEM((parts, FRAMES, elems, chan), jnp.bfloat16),
             pltpu.VMEM((beams * 2 * block, total), jnp.bfloat16),
             pltpu.VMEM((nchan, 2 * block, FRAMES * elems), jnp.bfloat16),

time: 14.8 us -> 14.6 us (0.986)
  Pallas kernels: 14 us -> 13.8 us
    pallas_call x1, Pallas kernels: 13.4 us -> 13.2 us  [on_device(): pl.pallas_call(functools.partial(main_kernel, nelem, nchan), in_specs=[pl...]
where the time goes in v5:
time: 14.6 us; the launch traced here: 14.4 us
  Pallas kernels  13.8 us (95%)
  between operations  0.64 us (4%)
    pallas_call x1, Pallas kernels, on_device(): pl.pallas_call(functools.partial(main_kernel, nelem, nchan), in_specs=[pl...  13.2 us
    pallas_call x1, Pallas kernels, on_device(): pl.pallas_call(deliver_kernel, in_specs=[pl.BlockSpec(memory_space=pl.ANY...  0.65 us

profile of v5, /device:TPU:0, one launch (start us, length us, event | category | flops | bytes accessed | tf_op | source)
XLA Modules:
  0.0 14.4 jit_solution(17626227686651203713)
XLA Ops:
  0.6 13.2 %shard_map.77 = (bf16[32,1024]{1,0:T(8,128)(2,1)S(1)}, f32[2,16,64]{2,1,0:T(8,128)S(1)}) custom-call(s32[32]{0:T(128)} %delay_hbm.1, s32[16]{0:T(128)} %map_hbm.1, bf16[2,32,19584]{2,1,0:T(8,128)(2,1)} %volt_hbm.1, bf16[16,1024]{1,0:T(8,128)(2,1)} %proto_hbm.1, bf16[64,2,4,1024]{3,2,1,0:T(4,128)(2,1)} %weight_hbm.1, bf16[8,256,256]{2,1,0:T(8,128)(2,1)} %constant.2.clone.basis_hbm), custom_call_target="tpu_custom_call" | custom-call | tf_op jit(solution)/shard_map/pallas_call | solution.py:400
  13.8 0.7 %shard_map.78 = (bf16[32,1024]{1,0:T(8,128)(2,1)}, f32[2,16,64]{2,1,0:T(8,128)}) custom-call(bf16[32,1024]{1,0:T(8,128)(2,1)S(1)} %get-tuple-element.4.power_from, f32[2,16,64]{2,1,0:T(8,128)S(1)} %get-tuple-element.5.beam_from), custom_call_target="tpu_custom_call" | custom-call | tf_op jit(solution)/shard_map/pallas_call | solution.py:428

commit v6 on v5

--- a/solution.py
+++ b/solution.py
@@ -204,8 +204,8 @@
         turns = wanted * (lane + j * LANES) + quarter
         real_basis.append(cosine(turns, chan))
         imag_basis.append(cosine(turns + 3 * (chan // 4), chan))
-    real_basis = split(jnp.concatenate(real_basis, axis=1))
-    imag_basis = split(jnp.concatenate(imag_basis, axis=1))
+    real_basis = jnp.concatenate(split(jnp.concatenate(real_basis, axis=1)), axis=0)
+    imag_basis = jnp.concatenate(split(jnp.concatenate(imag_basis, axis=1)), axis=0)
     proto_copy.wait()
     for t in range(taps):
         coef_ref[t] = jnp.broadcast_to(
@@ -223,6 +223,14 @@
         elif k + ahead == chunks:
             basis_copy.start()
             weight_copy.start()
+
+    def pick(r, basis):
+        return lax.dot_general(
+            basis,
+            wave_ref[r].reshape(frames * elems, chan),
+            NT,
+            preferred_element_type=jnp.float32,
+        )
 
     arrive(0)
     plan = turn_plan(0, groups, chunk_rows, delay_ref)
@@ -232,6 +240,8 @@
         if k + 1 < chunks:
             arrive(k + 1)
             plan = turn_plan(k + 1, groups, chunk_rows, delay_ref)
+        if k == groups:
+            both = pick(0, real_basis)
         for j in range(per):
             filter_column(k, groups, j, coef_ref, seg_ref, wave_ref)
             if k + 1 < chunks:
@@ -240,13 +250,8 @@
                 )
 
     wave = [wave_ref[r].reshape(frames * elems, chan) for r in range(2)]
-    chosen = jnp.zeros((rows, frames * elems), jnp.float32)
-    for r, basis in ((0, real_basis), (1, imag_basis)):
-        for piece in basis:
-            chosen = chosen + lax.dot_general(
-                piece, wave[r], NT, preferred_element_type=jnp.float32
-            )
-    chosen = chosen.astype(jnp.bfloat16)
+    both = both + pick(1, imag_basis)
+    chosen = (both[:rows] + both[rows:]).astype(jnp.bfloat16)
     for c in range(nchan):
         send_ref[c] = chosen[2 * block * c : 2 * block * (c + 1)]
 

time: 14.6 us -> 14.5 us (level)
  no operation moved by 1% of the time
where the time goes in v6:
time: 14.5 us; the launch traced here: 14.4 us
  Pallas kernels  13.8 us (95%)
  between operations  0.64 us (4%)
    pallas_call x1, Pallas kernels, on_device(): pl.pallas_call(functools.partial(main_kernel, nelem, nchan), in_specs=[pl...  13.1 us
    pallas_call x1, Pallas kernels, on_device(): pl.pallas_call(deliver_kernel, in_specs=[pl.BlockSpec(memory_space=pl.ANY...  0.65 us

profile of v6, /device:TPU:0, one launch (start us, length us, event | category | flops | bytes accessed | tf_op | source)
XLA Modules:
  0.0 14.4 jit_solution(10767765558349984862)
XLA Ops:
  0.6 13.1 %shard_map.77 = (bf16[32,1024]{1,0:T(8,128)(2,1)S(1)}, f32[2,16,64]{2,1,0:T(8,128)S(1)}) custom-call(s32[32]{0:T(128)} %delay_hbm.1, s32[16]{0:T(128)} %map_hbm.1, bf16[2,32,19584]{2,1,0:T(8,128)(2,1)} %volt_hbm.1, bf16[16,1024]{1,0:T(8,128)(2,1)} %proto_hbm.1, bf16[64,2,4,1024]{3,2,1,0:T(4,128)(2,1)} %weight_hbm.1, bf16[8,256,256]{2,1,0:T(8,128)(2,1)} %constant.2.clone.basis_hbm), custom_call_target="tpu_custom_call" | custom-call | tf_op jit(solution)/shard_map/pallas_call | solution.py:405
  13.8 0.7 %shard_map.78 = (bf16[32,1024]{1,0:T(8,128)(2,1)}, f32[2,16,64]{2,1,0:T(8,128)}) custom-call(bf16[32,1024]{1,0:T(8,128)(2,1)S(1)} %get-tuple-element.4.power_from, f32[2,16,64]{2,1,0:T(8,128)S(1)} %get-tuple-element.5.beam_from), custom_call_target="tpu_custom_call" | custom-call | tf_op jit(solution)/shard_map/pallas_call | solution.py:433
